TPU v7x, 32 devices: a whole 2x2x4 slice. The times are simulated.
32 devices in a mesh: pipe: 2 (over x), tensor: 4 (over y, core), expert: 4 (over z).
Axes of the slice: x: 2, y: 2, z: 4, core: 2. Of those that a mesh axis runs over, the one named last changes fastest.
Arguments:
- tokens: bfloat16 [2, 256, 4096], P(None, 'expert'), may hold values from -6 to 6
- gains: float32 [2, 4096], P('pipe'), may hold values from 0.1 to 1.9
- route_ids: int32 [2, 2, 256, 2], P('pipe', None, 'expert'), may hold values from 0 to 3, all different within a row
- route_weights: float32 [2, 2, 256, 2], P('pipe', None, 'expert'), may hold values from 0.2 to 1
- picks: int32 [2, 2, 4, 64], P('pipe', None, 'expert'), may hold values from 0 to 63, each once within a row
- w_gate: bfloat16 [2, 4, 4096, 1536], P('pipe', 'expert', None, 'tensor'), may hold values from -0.09375 to 0.09375
- w_up: bfloat16 [2, 4, 4096, 1536], P('pipe', 'expert', None, 'tensor'), may hold values from -0.09375 to 0.09375
- w_down: bfloat16 [2, 4, 1536, 4096], P('pipe', 'expert', 'tensor'), may hold values from -0.15625 to 0.15625
Outputs:
- streams: bfloat16 [2, 2, 256, 4096], P('pipe', None, 'expert', 'tensor')
Inputs may be any that keep to these rules, and one draw needn't show every extreme that they name: `route_ids`: each token names 2 different experts; every expert is named by some token. `picks`: for every layer, micro-batch and block of 64 tokens, a permutation of 0 to 63.
All inputs are finite; a program needn't handle non-finite values.
Results may differ from a plain program's by a relative error of at most 0.025.
Values may be sent and summed in bfloat16 or wider, within the bound.
A program may use at most 64 MiB of HBM per device.

v0:
```python
import jax
import jax.numpy as jnp
from jax import lax
from jax.sharding import PartitionSpec as P

epsilon = 1e-06


def passed_along(block, axis, distance):
    devices = range(lax.axis_size(axis))
    route = [(i - distance, i) for i in devices if i - distance in devices]
    return lax.ppermute(block, axis, route)


def local(tokens, gains, route_ids, route_weights, picks, w_gate, w_up, w_down):
    micro_count = tokens.shape[0]
    local_tokens = tokens.shape[1]
    model_width = tokens.shape[2]
    route_count = route_ids.shape[3]
    tensor_ranks = lax.axis_size("tensor")
    groups = lax.axis_size("expert")
    sections = lax.axis_size("pipe")
    quarter = local_tokens // tensor_ranks
    capacity = 4 * quarter * route_count // (3 * groups)
    slice_width = model_width // tensor_ranks
    my_section = lax.axis_index("pipe")
    my_rank = lax.axis_index("tensor")
    gain_row = gains[0]
    gate_matrix = w_gate[0, 0]
    up_matrix = w_up[0, 0]
    down_matrix = w_down[0, 0]

    def expert_work(arrived):
        gathered = lax.all_gather(arrived, "tensor", axis=0, tiled=True)
        row_count = gathered.shape[0] * gathered.shape[1]
        row_block = gathered.reshape(row_count, model_width)
        gate_val = jnp.dot(row_block, gate_matrix, preferred_element_type=jnp.float32)
        up_val = jnp.dot(row_block, up_matrix, preferred_element_type=jnp.float32)
        hidden = (jax.nn.silu(gate_val) * up_val).astype(jnp.bfloat16)
        partial_sum = jnp.dot(hidden, down_matrix, preferred_element_type=jnp.float32)
        summed = lax.psum_scatter(
            partial_sum.reshape(gathered.shape).astype(jnp.bfloat16),
            "tensor",
            scatter_dimension=0,
            tiled=True,
        )
        return summed

    def expert_layer(quarter_rows, chosen, micro_index):
        section_ids = route_ids[0, micro_index][chosen]
        section_weights = route_weights[0, micro_index][chosen]
        stream_f = quarter_rows.astype(jnp.float32)
        inv_rms = lax.rsqrt(jnp.mean(stream_f * stream_f, axis=1, keepdims=True) + epsilon)
        normed = (stream_f * inv_rms * gain_row[None, :]).astype(jnp.bfloat16)
        flat_ids = section_ids.reshape(-1)
        onehot = (flat_ids[:, None] == jnp.arange(groups, dtype=jnp.int32)[None, :]).astype(
            jnp.int32
        )
        earlier = jnp.cumsum(onehot, axis=0) - onehot
        slot_index = jnp.sum(earlier * onehot, axis=1)
        kept_mask = slot_index < capacity
        target = jnp.where(kept_mask, flat_ids * capacity + slot_index, groups * capacity)
        placing = (
            jnp.arange(groups * capacity, dtype=jnp.int32)[:, None] == target[None, :]
        ).astype(jnp.bfloat16)
        routed = jnp.repeat(normed, route_count, axis=0)
        outgoing = jnp.dot(placing, routed, preferred_element_type=jnp.float32).astype(jnp.bfloat16)
        outgoing = outgoing.reshape(groups, capacity, model_width)
        returned = expert_work(
            lax.all_to_all(outgoing, "expert", split_axis=0, concat_axis=0, tiled=True)
        )
        homeward = lax.all_to_all(returned, "expert", split_axis=0, concat_axis=0, tiled=True)
        flat_back = jnp.concatenate(
            [
                homeward.reshape(groups * capacity, model_width),
                jnp.zeros((1, model_width), jnp.bfloat16),
            ],
            axis=0,
        )
        picked = flat_back[target].astype(jnp.float32).reshape(quarter, route_count, model_width)
        kept_grid = kept_mask.reshape(quarter, route_count)
        weighted = picked * (section_weights * kept_grid)[..., None]
        update = jnp.sum(weighted, axis=1)
        return (stream_f + update).astype(jnp.bfloat16)

    def run_section(stream, micro_index):
        order_all = picks[0, micro_index, 0]
        chosen = lax.dynamic_slice_in_dim(order_all, my_rank * quarter, quarter)
        permuted = stream[order_all]
        quarter_rows = lax.all_to_all(permuted, "tensor", split_axis=0, concat_axis=1, tiled=True)
        fresh_rows = expert_layer(quarter_rows, chosen, micro_index)
        spread = lax.all_to_all(fresh_rows, "tensor", split_axis=1, concat_axis=0, tiled=True)
        return jnp.zeros_like(stream).at[order_all].set(spread)

    def first_input(micro_index):
        whole = tokens[micro_index]
        return lax.dynamic_slice_in_dim(whole, my_rank * slice_width, slice_width, 1)

    def send_on(fresh):
        return passed_along(fresh, "pipe", 1)

    def section_tick(carry, tick_index):
        arrived, collected = carry
        micro_index = tick_index - my_section
        active = (micro_index >= 0) & (micro_index < micro_count)
        clipped = jnp.clip(micro_index, 0, micro_count - 1)
        stream = jnp.where(my_section == 0, first_input(clipped), arrived)
        computed = run_section(stream, clipped)
        fresh = jnp.where(active, computed, stream)
        written = collected.at[clipped].set(fresh)
        collected = jnp.where(active, written, collected)
        return ((send_on(fresh), collected), None)

    empty_state = jnp.zeros((local_tokens, slice_width), jnp.bfloat16)
    collected = jnp.zeros((micro_count, local_tokens, slice_width), jnp.bfloat16)
    ticks = jnp.arange(micro_count + sections - 1, dtype=jnp.int32)
    (final_state, collected), unused = lax.scan(section_tick, (empty_state, collected), ticks)
    return collected[None]


def solution(mesh):
    return jax.shard_map(
        local,
        mesh=mesh,
        in_specs=(
            P(None, "expert", None),
            P("pipe", None),
            P("pipe", None, "expert", None),
            P("pipe", None, "expert", None),
            P("pipe", None, "expert", None),
            P("pipe", "expert", None, "tensor"),
            P("pipe", "expert", None, "tensor"),
            P("pipe", "expert", "tensor", None),
        ),
        out_specs=P("pipe", None, "expert", "tensor"),
        check_vma=False,
    )
```

profile of v0, /device:TPU:0, one launch (start us, length us, event | category | flops | bytes accessed | tf_op | source)
XLA Modules:
  0.0 413.7 jit_solution(168059890202536682)
XLA Ops:
  6.6 399.6 %while.16 = (s32[]{:T(128)}, bf16[64,1024]{1,0:T(8,128)(2,1)S(1)}, bf16[2,64,1024]{2,1,0:T(8,128)(2,1)S(1)}, s32[3]{0:T(128)S(1)}, s32[]{:T(128)}, /*index=5*/s3...) while((s32[]{:T(128)}, bf16[64,1024]{1,0:T(8,128)(2,1)S(1)}, ...), condition=%wide.region_8.9_spmd, body=%wide.region_0.8_spmd.sunk | while | flops 1522746880 | bytes 43274836 | solution.py:117
  10.9 4.3 %all-to-all-start = ((bf16[4,16,1024]{2,1,0:T(8,128)(2,1)}), bf16[4,16,1024]{2,1,0:T(8,128)(2,1)S(1)}, u32[]{:S(2)}, u32[]{:S(2)}) async-start(bf16[4,16,1024]{2,1,0:T(8,128)(2,1)} %bitcast.115), calls=%async_computation | async-start | bytes 262144 | tf_op jit(solution)/shard_map/while/body/eval_jaxpr/all_to_all | solution.py:90
  21.5 19.4 %all_to_all.72 = bf16[4,10,4096]{2,1,0:T(8,128)(2,1)} all-to-all(bf16[4,10,4096]{2,1,0:T(8,128)(2,1)S(1)} %reshape.338), channel_id=1, replica_groups=mesh['pipe'=2,'tensor'=4,'expert'=4] {'expert'}, dimensions={0} | all-to-all | bytes 655360 | tf_op jit(solution)/shard_map/while/body/eval_jaxpr/all_to_all | solution.py:70
  40.9 21.1 %all-gather.2.cloned.1.call-done = bf16[16,10,4096]{2,1,0:T(8,128)(2,1)} async-done(((bf16[4,10,4096]{2,1,0:T(8,128)(2,1)}), bf16[16,10,4096]{2,1,0:T(8,128)(2,1)}) %all-gather.2.cloned.1.call-update) | async-done | bytes 1310736 | tf_op jit(solution)/shard_map/while/body/eval_jaxpr/all_gather | solution.py:34
  66.6 4.5 %convolution_convert_fusion.5 = bf16[160,4096]{1,0:T(8,128)(2,1)S(1)} fusion(bf16[384,4096]{1,0:T(8,128)(2,1)} %get-tuple-element.469, bf16[160,4096]{1,0:T(8,128)(2,1)S(1)} %reshape.339, bf16[4096,384]{1,0:T(8,128)(2,1)} %get-tuple-element.468, f32[160,384]{1,0:T(8,128)S(1)} %fusion.60), kind=kOutput, calls=%fused_computation.5.clone.1 | convolution fusion | flops 1007656960 | bytes 9158656 | tf_op jit(solution)/shard_map/while/body/eval_jaxpr/dot_general | solution.py:40
  73.6 30.5 %reduce-scatter.2.cloned.1.call-done = bf16[4,10,4096]{2,1,0:T(8,128)(2,1)} async-done(((bf16[16,10,4096]{2,1,0:T(8,128)(2,1)}), bf16[4,10,4096]{2,1,0:T(8,128)(2,1)}) %reduce-scatter.2.cloned.1.call-update) | async-done | bytes 327696 | tf_op jit(solution)/shard_map/while/body/eval_jaxpr/reduce_scatter | solution.py:41
  104.1 4.6 %all-to-all-start.2 = ((bf16[4,10,4096]{2,1,0:T(8,128)(2,1)}), bf16[4,10,4096]{2,1,0:T(8,128)(2,1)S(1)}, u32[]{:S(2)}, u32[]{:S(2)}) async-start(bf16[4,10,4096]{2,1,0:T(8,128)(2,1)} %reduce-scatter.2.cloned.1.call-done), calls=%async_computation.3 | async-start | bytes 1048576 | tf_op jit(solution)/shard_map/while/body/eval_jaxpr/all_to_all | solution.py:72
  108.7 14.3 %all-to-all-done.2 = bf16[4,10,4096]{2,1,0:T(8,128)(2,1)S(1)} async-done(((bf16[4,10,4096]{2,1,0:T(8,128)(2,1)}), bf16[4,10,4096]{2,1,0:T(8,128)(2,1)S(1)}, u32[]{:S(2)}, u32[]{:S(2)}) %all-to-all-start.2) | async-done | bytes 327712 | tf_op jit(solution)/shard_map/while/body/eval_jaxpr/all_to_all | solution.py:72
  125.6 3.3 all-to-all-start.3
  129.8 3.8 all-to-all-done.3
  135.2 3.4 collective-permute-start
  145.4 3.3 all-to-all-start
  155.0 17.5 %all_to_all.72 = bf16[4,10,4096]{2,1,0:T(8,128)(2,1)} all-to-all(bf16[4,10,4096]{2,1,0:T(8,128)(2,1)S(1)} %reshape.338), channel_id=1, replica_groups=mesh['pipe'=2,'tensor'=4,'expert'=4] {'expert'}, dimensions={0} | all-to-all | bytes 655360 | tf_op jit(solution)/shard_map/while/body/eval_jaxpr/all_to_all | solution.py:70
  172.6 22.0 %all-gather.2.cloned.1.call-done = bf16[16,10,4096]{2,1,0:T(8,128)(2,1)} async-done(((bf16[4,10,4096]{2,1,0:T(8,128)(2,1)}), bf16[16,10,4096]{2,1,0:T(8,128)(2,1)}) %all-gather.2.cloned.1.call-update) | async-done | bytes 1310736 | tf_op jit(solution)/shard_map/while/body/eval_jaxpr/all_gather | solution.py:34
  196.4 2.7 fusion.60
  199.1 4.5 %convolution_convert_fusion.5 = bf16[160,4096]{1,0:T(8,128)(2,1)S(1)} fusion(bf16[384,4096]{1,0:T(8,128)(2,1)} %get-tuple-element.469, bf16[160,4096]{1,0:T(8,128)(2,1)S(1)} %reshape.339, bf16[4096,384]{1,0:T(8,128)(2,1)} %get-tuple-element.468, f32[160,384]{1,0:T(8,128)S(1)} %fusion.60), kind=kOutput, calls=%fused_computation.5.clone.1 | convolution fusion | flops 1007656960 | bytes 9158656 | tf_op jit(solution)/shard_map/while/body/eval_jaxpr/dot_general | solution.py:40
  206.2 30.5 %reduce-scatter.2.cloned.1.call-done = bf16[4,10,4096]{2,1,0:T(8,128)(2,1)} async-done(((bf16[16,10,4096]{2,1,0:T(8,128)(2,1)}), bf16[4,10,4096]{2,1,0:T(8,128)(2,1)}) %reduce-scatter.2.cloned.1.call-update) | async-done | bytes 327696 | tf_op jit(solution)/shard_map/while/body/eval_jaxpr/reduce_scatter | solution.py:41
  236.6 4.6 %all-to-all-start.2 = ((bf16[4,10,4096]{2,1,0:T(8,128)(2,1)}), bf16[4,10,4096]{2,1,0:T(8,128)(2,1)S(1)}, u32[]{:S(2)}, u32[]{:S(2)}) async-start(bf16[4,10,4096]{2,1,0:T(8,128)(2,1)} %reduce-scatter.2.cloned.1.call-done), calls=%async_computation.3 | async-start | bytes 1048576 | tf_op jit(solution)/shard_map/while/body/eval_jaxpr/all_to_all | solution.py:72
  241.3 14.3 %all-to-all-done.2 = bf16[4,10,4096]{2,1,0:T(8,128)(2,1)S(1)} async-done(((bf16[4,10,4096]{2,1,0:T(8,128)(2,1)}), bf16[4,10,4096]{2,1,0:T(8,128)(2,1)S(1)}, u32[]{:S(2)}, u32[]{:S(2)}) %all-to-all-start.2) | async-done | bytes 327712 | tf_op jit(solution)/shard_map/while/body/eval_jaxpr/all_to_all | solution.py:72
  258.2 3.3 all-to-all-start.3
  262.3 3.8 all-to-all-done.3
  267.8 3.4 collective-permute-start
  277.9 3.3 all-to-all-start
  287.5 17.5 %all_to_all.72 = bf16[4,10,4096]{2,1,0:T(8,128)(2,1)} all-to-all(bf16[4,10,4096]{2,1,0:T(8,128)(2,1)S(1)} %reshape.338), channel_id=1, replica_groups=mesh['pipe'=2,'tensor'=4,'expert'=4] {'expert'}, dimensions={0} | all-to-all | bytes 655360 | tf_op jit(solution)/shard_map/while/body/eval_jaxpr/all_to_all | solution.py:70
  305.1 22.0 %all-gather.2.cloned.1.call-done = bf16[16,10,4096]{2,1,0:T(8,128)(2,1)} async-done(((bf16[4,10,4096]{2,1,0:T(8,128)(2,1)}), bf16[16,10,4096]{2,1,0:T(8,128)(2,1)}) %all-gather.2.cloned.1.call-update) | async-done | bytes 1310736 | tf_op jit(solution)/shard_map/while/body/eval_jaxpr/all_gather | solution.py:34
  331.7 4.5 %convolution_convert_fusion.5 = bf16[160,4096]{1,0:T(8,128)(2,1)S(1)} fusion(bf16[384,4096]{1,0:T(8,128)(2,1)} %get-tuple-element.469, bf16[160,4096]{1,0:T(8,128)(2,1)S(1)} %reshape.339, bf16[4096,384]{1,0:T(8,128)(2,1)} %get-tuple-element.468, f32[160,384]{1,0:T(8,128)S(1)} %fusion.60), kind=kOutput, calls=%fused_computation.5.clone.1 | convolution fusion | flops 1007656960 | bytes 9158656 | tf_op jit(solution)/shard_map/while/body/eval_jaxpr/dot_general | solution.py:40
  338.7 30.5 %reduce-scatter.2.cloned.1.call-done = bf16[4,10,4096]{2,1,0:T(8,128)(2,1)} async-done(((bf16[16,10,4096]{2,1,0:T(8,128)(2,1)}), bf16[4,10,4096]{2,1,0:T(8,128)(2,1)}) %reduce-scatter.2.cloned.1.call-update) | async-done | bytes 327696 | tf_op jit(solution)/shard_map/while/body/eval_jaxpr/reduce_scatter | solution.py:41
  369.2 4.6 %all-to-all-start.2 = ((bf16[4,10,4096]{2,1,0:T(8,128)(2,1)}), bf16[4,10,4096]{2,1,0:T(8,128)(2,1)S(1)}, u32[]{:S(2)}, u32[]{:S(2)}) async-start(bf16[4,10,4096]{2,1,0:T(8,128)(2,1)} %reduce-scatter.2.cloned.1.call-done), calls=%async_computation.3 | async-start | bytes 1048576 | tf_op jit(solution)/shard_map/while/body/eval_jaxpr/all_to_all | solution.py:72
  373.8 14.3 %all-to-all-done.2 = bf16[4,10,4096]{2,1,0:T(8,128)(2,1)S(1)} async-done(((bf16[4,10,4096]{2,1,0:T(8,128)(2,1)}), bf16[4,10,4096]{2,1,0:T(8,128)(2,1)S(1)}, u32[]{:S(2)}, u32[]{:S(2)}) %all-to-all-start.2) | async-done | bytes 327712 | tf_op jit(solution)/shard_map/while/body/eval_jaxpr/all_to_all | solution.py:72
  390.7 3.3 all-to-all-start.3
  394.8 3.8 all-to-all-done.3
  400.3 3.4 collective-permute-start
  (172 shorter events, 71.3 us)
Async XLA Ops:
  10.9 8.9 %all-to-all-start = ((bf16[4,16,1024]{2,1,0:T(8,128)(2,1)}), bf16[4,16,1024]{2,1,0:T(8,128)(2,1)S(1)}, u32[]{:S(2)}, u32[]{:S(2)}) async-start(bf16[4,16,1024]{2,1,0:T(8,128)(2,1)} %bitcast.115), calls=%async_computation | async-start | bytes 262144 | tf_op jit(solution)/shard_map/while/body/eval_jaxpr/all_to_all | solution.py:90
  15.2 46.9 %all-gather.2.cloned.1.call-start = ((), (), s32[]{:S(2)}) async-start(), calls=%async_computation.5 | async-start | bytes 2621440 | tf_op jit(solution)/shard_map/while/body/eval_jaxpr/all_gather | solution.py:34
  40.9 63.2 %reduce-scatter.2.cloned.1.call-start = ((), (), s32[]{:S(2)}) async-start(), calls=%async_computation.6 | async-start | bytes 2621440 | tf_op jit(solution)/shard_map/while/body/eval_jaxpr/reduce_scatter | solution.py:41
  71.1 1.8 copy-start.1
  104.1 18.9 %all-to-all-start.2 = ((bf16[4,10,4096]{2,1,0:T(8,128)(2,1)}), bf16[4,10,4096]{2,1,0:T(8,128)(2,1)S(1)}, u32[]{:S(2)}, u32[]{:S(2)}) async-start(bf16[4,10,4096]{2,1,0:T(8,128)(2,1)} %reduce-scatter.2.cloned.1.call-done), calls=%async_computation.3 | async-start | bytes 1048576 | tf_op jit(solution)/shard_map/while/body/eval_jaxpr/all_to_all | solution.py:72
  108.7 20.3 %copy-start.2 = (s32[3]{0:T(128)S(1)}, s32[3]{0:T(128)}, u32[]{:S(2)}) copy-start(s32[3]{0:T(128)} %get-tuple-element.473) | copy-start | bytes 40 | tf_op jit(solution)/shard_map/while
  125.6 7.9 %all-to-all-start.3 = ((bf16[16,4,1024]{2,0,1:T(8,128)(2,1)}), bf16[16,4,1024]{2,0,1:T(8,128)(2,1)S(1)}, u32[]{:S(2)}, u32[]{:S(2)}) async-start(bf16[16,4,1024]{2,0,1:T(8,128)(2,1)} %fusion.63), calls=%async_computation.4 | async-start | bytes 262144 | tf_op jit(solution)/shard_map/while/body/eval_jaxpr/all_to_all | solution.py:92
  135.2 5.9 %collective-permute-start = (bf16[64,1024]{1,0:T(8,128)(2,1)S(1)}, bf16[64,1024]{1,0:T(8,128)(2,1)S(1)}, u32[]{:S(2)}, u32[]{:S(2)}) collective-permute-start(bf16[64,1024]{1,0:T(8,128)(2,1)S(1)} %get-tuple-element.409), channel_id=1, source_target_pairs={{0,16},{1,17},{2,18},{3,19},{4,20},{5,21},{6,22},{7,23},{8,24},{9,... | collective-permute-start | bytes 393224 | tf_op jit(solution)/shard_map/while/body/eval_jaxpr/ppermute | solution.py:12
  145.4 7.9 %all-to-all-start = ((bf16[4,16,1024]{2,1,0:T(8,128)(2,1)}), bf16[4,16,1024]{2,1,0:T(8,128)(2,1)S(1)}, u32[]{:S(2)}, u32[]{:S(2)}) async-start(bf16[4,16,1024]{2,1,0:T(8,128)(2,1)} %bitcast.115), calls=%async_computation | async-start | bytes 262144 | tf_op jit(solution)/shard_map/while/body/eval_jaxpr/all_to_all | solution.py:90
  148.7 45.9 %all-gather.2.cloned.1.call-start = ((), (), s32[]{:S(2)}) async-start(), calls=%async_computation.5 | async-start | bytes 2621440 | tf_op jit(solution)/shard_map/while/body/eval_jaxpr/all_gather | solution.py:34
  172.5 64.1 %reduce-scatter.2.cloned.1.call-start = ((), (), s32[]{:S(2)}) async-start(), calls=%async_computation.6 | async-start | bytes 2621440 | tf_op jit(solution)/shard_map/while/body/eval_jaxpr/reduce_scatter | solution.py:41
  203.6 1.8 copy-start.1
  236.6 18.9 %all-to-all-start.2 = ((bf16[4,10,4096]{2,1,0:T(8,128)(2,1)}), bf16[4,10,4096]{2,1,0:T(8,128)(2,1)S(1)}, u32[]{:S(2)}, u32[]{:S(2)}) async-start(bf16[4,10,4096]{2,1,0:T(8,128)(2,1)} %reduce-scatter.2.cloned.1.call-done), calls=%async_computation.3 | async-start | bytes 1048576 | tf_op jit(solution)/shard_map/while/body/eval_jaxpr/all_to_all | solution.py:72
  241.3 20.2 %copy-start.2 = (s32[3]{0:T(128)S(1)}, s32[3]{0:T(128)}, u32[]{:S(2)}) copy-start(s32[3]{0:T(128)} %get-tuple-element.473) | copy-start | bytes 40 | tf_op jit(solution)/shard_map/while
  258.2 7.9 %all-to-all-start.3 = ((bf16[16,4,1024]{2,0,1:T(8,128)(2,1)}), bf16[16,4,1024]{2,0,1:T(8,128)(2,1)S(1)}, u32[]{:S(2)}, u32[]{:S(2)}) async-start(bf16[16,4,1024]{2,0,1:T(8,128)(2,1)} %fusion.63), calls=%async_computation.4 | async-start | bytes 262144 | tf_op jit(solution)/shard_map/while/body/eval_jaxpr/all_to_all | solution.py:92
  267.8 5.9 %collective-permute-start = (bf16[64,1024]{1,0:T(8,128)(2,1)S(1)}, bf16[64,1024]{1,0:T(8,128)(2,1)S(1)}, u32[]{:S(2)}, u32[]{:S(2)}) collective-permute-start(bf16[64,1024]{1,0:T(8,128)(2,1)S(1)} %get-tuple-element.409), channel_id=1, source_target_pairs={{0,16},{1,17},{2,18},{3,19},{4,20},{5,21},{6,22},{7,23},{8,24},{9,... | collective-permute-start | bytes 393224 | tf_op jit(solution)/shard_map/while/body/eval_jaxpr/ppermute | solution.py:12
  277.9 7.9 %all-to-all-start = ((bf16[4,16,1024]{2,1,0:T(8,128)(2,1)}), bf16[4,16,1024]{2,1,0:T(8,128)(2,1)S(1)}, u32[]{:S(2)}, u32[]{:S(2)}) async-start(bf16[4,16,1024]{2,1,0:T(8,128)(2,1)} %bitcast.115), calls=%async_computation | async-start | bytes 262144 | tf_op jit(solution)/shard_map/while/body/eval_jaxpr/all_to_all | solution.py:90
  281.3 45.9 %all-gather.2.cloned.1.call-start = ((), (), s32[]{:S(2)}) async-start(), calls=%async_computation.5 | async-start | bytes 2621440 | tf_op jit(solution)/shard_map/while/body/eval_jaxpr/all_gather | solution.py:34
  305.1 64.1 %reduce-scatter.2.cloned.1.call-start = ((), (), s32[]{:S(2)}) async-start(), calls=%async_computation.6 | async-start | bytes 2621440 | tf_op jit(solution)/shard_map/while/body/eval_jaxpr/reduce_scatter | solution.py:41
  336.2 1.8 copy-start.1
  369.2 18.9 %all-to-all-start.2 = ((bf16[4,10,4096]{2,1,0:T(8,128)(2,1)}), bf16[4,10,4096]{2,1,0:T(8,128)(2,1)S(1)}, u32[]{:S(2)}, u32[]{:S(2)}) async-start(bf16[4,10,4096]{2,1,0:T(8,128)(2,1)} %reduce-scatter.2.cloned.1.call-done), calls=%async_computation.3 | async-start | bytes 1048576 | tf_op jit(solution)/shard_map/while/body/eval_jaxpr/all_to_all | solution.py:72
  373.8 20.2 %copy-start.2 = (s32[3]{0:T(128)S(1)}, s32[3]{0:T(128)}, u32[]{:S(2)}) copy-start(s32[3]{0:T(128)} %get-tuple-element.473) | copy-start | bytes 40 | tf_op jit(solution)/shard_map/while
  390.7 7.9 %all-to-all-start.3 = ((bf16[16,4,1024]{2,0,1:T(8,128)(2,1)}), bf16[16,4,1024]{2,0,1:T(8,128)(2,1)S(1)}, u32[]{:S(2)}, u32[]{:S(2)}) async-start(bf16[16,4,1024]{2,0,1:T(8,128)(2,1)} %fusion.63), calls=%async_computation.4 | async-start | bytes 262144 | tf_op jit(solution)/shard_map/while/body/eval_jaxpr/all_to_all | solution.py:92
  400.3 5.9 %collective-permute-start = (bf16[64,1024]{1,0:T(8,128)(2,1)S(1)}, bf16[64,1024]{1,0:T(8,128)(2,1)S(1)}, u32[]{:S(2)}, u32[]{:S(2)}) collective-permute-start(bf16[64,1024]{1,0:T(8,128)(2,1)S(1)} %get-tuple-element.409), channel_id=1, source_target_pairs={{0,16},{1,17},{2,18},{3,19},{4,20},{5,21},{6,22},{7,23},{8,24},{9,... | collective-permute-start | bytes 393224 | tf_op jit(solution)/shard_map/while/body/eval_jaxpr/ppermute | solution.py:12
  406.2 0.7 copy-start
Sparse Core Ops, SparseCore 0:
  41.0 20.9 all-gather.1
  72.8 31.2 reduce-scatter.1
  172.6 21.9 all-gather.1
  205.4 31.1 reduce-scatter.1
  305.2 21.9 all-gather.1
  337.9 31.1 reduce-scatter.1
where the time goes:
time: 415 us; the launch traced here: 414 us
  waiting for transfers between devices  224 us (54%)
  blocking collectives  54.4 us (13%)
  starting transfers between devices  45 us (11%)
  local copies, waits for them, and re-layouts  31.1 us (7%)
  matrix products  22.4 us (5%)
  other arithmetic  20.1 us (5%)
  between operations  13.4 us (3%)
    reduce_scatter x3, waiting for transfers between devices, expert_work(): lax.psum_scatter(partial_sum.reshape(gathered.shape).astype(jnp.bfloat16)...  91.4 us
    all_gather x3, waiting for transfers between devices, expert_work(): gathered = lax.all_gather(arrived, 'tensor', axis=0, tiled=True)  65.2 us
    all_to_all x3, blocking collectives, expert_layer(): lax.all_to_all(outgoing, 'expert', split_axis=0, concat_axis=0, tiled=True)  54.4 us
    all_to_all x3, waiting for transfers between devices, expert_layer(): lax.all_to_all(returned, 'expert', split_axis=0, concat_axis=0, tiled=True)  42.9 us
    all_to_all x3, starting transfers between devices, expert_layer(): lax.all_to_all(returned, 'expert', split_axis=0, concat_axis=0, tiled=True)  13.8 us
    dot_general x3, matrix products, expert_work(): jnp.dot(hidden, down_matrix, preferred_element_type=jnp.float32)  13.5 us
    all_to_all x3, waiting for transfers between devices, run_section(): lax.all_to_all(fresh_rows, 'tensor', split_axis=1, concat_axis=0, tiled=T...  11.3 us
    all_to_all x3, starting transfers between devices, run_section(): lax.all_to_all(permuted, 'tensor', split_axis=0, concat_axis=1, tiled=True)  10.9 us
  transfers between devices with their start and end apart: 18, of which 18 were waited for; matrix products, arithmetic and copies ran while one was open for 3% of the time, Pallas kernels for 0%

commit v1 on v0

--- a/solution.py
+++ b/solution.py
@@ -31,7 +31,16 @@
     down_matrix = w_down[0, 0]
 
     def expert_work(arrived):
-        gathered = lax.all_gather(arrived, "tensor", axis=0, tiled=True)
+        ring = [arrived]
+        for hop in range(3):
+            ring.append(
+                lax.ppermute(ring[-1], "tensor", [(dev, (dev + 1) % 4) for dev in range(4)])
+            )
+        gathered = jnp.roll(
+            jnp.concatenate(ring[::-1], axis=0),
+            (lax.axis_index("tensor") + 1) * ring[0].shape[0],
+            axis=0,
+        )
         row_count = gathered.shape[0] * gathered.shape[1]
         row_block = gathered.reshape(row_count, model_width)
         gate_val = jnp.dot(row_block, gate_matrix, preferred_element_type=jnp.float32)

time: 415 us -> 425 us (1.024)
  waiting for transfers between devices: 224 us -> 236 us
    ppermute x0 -> x9, waiting for transfers between devices: none -> 77.4 us  [expert_work(): lax.ppermute(ring[-1], 'tensor', [(dev, (dev + 1) % 4) for dev in range(4)])]
    all_gather x3 -> x0, waiting for transfers between devices: 65.2 us -> none  [expert_work(): gathered = lax.all_gather(arrived, 'tensor', axis=0, tiled=True)]
  transfers between devices with their start and end apart: 18 -> 24, of which waited for: 18 -> 24; matrix products, arithmetic and copies ran while one was open for 3% -> 2% of each run, Pallas kernels for 0% -> 0%
where the time goes in v1:
time: 425 us; the launch traced here: 423 us
  waiting for transfers between devices  236 us (56%)
  blocking collectives  52.9 us (12%)
  starting transfers between devices  44.9 us (11%)
  local copies, waits for them, and re-layouts  31 us (7%)
  matrix products  22.4 us (5%)
  other arithmetic  19.7 us (5%)
  between operations  13.1 us (3%)
    reduce_scatter x3, waiting for transfers between devices, expert_work(): lax.psum_scatter(partial_sum.reshape(gathered.shape).astype(jnp.bfloat16)...  88.5 us
    ppermute x9, waiting for transfers between devices, expert_work(): lax.ppermute(ring[-1], 'tensor', [(dev, (dev + 1) % 4) for dev in range(4)])  77.4 us
    all_to_all x3, blocking collectives, expert_layer(): lax.all_to_all(outgoing, 'expert', split_axis=0, concat_axis=0, tiled=True)  52.9 us
    all_to_all x3, waiting for transfers between devices, expert_layer(): lax.all_to_all(returned, 'expert', split_axis=0, concat_axis=0, tiled=True)  42.8 us
    all_to_all x3, starting transfers between devices, expert_layer(): lax.all_to_all(returned, 'expert', split_axis=0, concat_axis=0, tiled=True)  13.8 us
    dot_general x3, matrix products, expert_work(): jnp.dot(hidden, down_matrix, preferred_element_type=jnp.float32)  13.5 us
    all_to_all x3, waiting for transfers between devices, run_section(): lax.all_to_all(fresh_rows, 'tensor', split_axis=1, concat_axis=0, tiled=T...  11.5 us
    all_to_all x3, starting transfers between devices, run_section(): lax.all_to_all(permuted, 'tensor', split_axis=0, concat_axis=1, tiled=True)  10.9 us
  transfers between devices with their start and end apart: 24, of which 24 were waited for; matrix products, arithmetic and copies ran while one was open for 2% of the time, Pallas kernels for 0%

profile of v1, /device:TPU:0, one launch (start us, length us, event | category | flops | bytes accessed | tf_op | source)
XLA Modules:
  0.0 423.3 jit_solution(8404512888262546757)
XLA Ops:
  7.8 409.0 %while.16 = (s32[]{:T(128)}, bf16[64,1024]{1,0:T(8,128)(2,1)S(1)}, bf16[2,64,1024]{2,1,0:T(8,128)(2,1)}, s32[3]{0:T(128)}, s32[]{:T(128)}, /*index=5*/s32[1,2,1,...) while((s32[]{:T(128)}, bf16[64,1024]{1,0:T(8,128)(2,1)S(1)}, ...), condition=%wide.region_8.9_spmd, body=%wide.region_0.8_spmd.sunk | while | flops 1522746880 | bytes 55269456 | solution.py:126
  13.4 4.3 %all-to-all-start = ((bf16[4,16,1024]{2,1,0:T(8,128)(2,1)}), bf16[4,16,1024]{2,1,0:T(8,128)(2,1)S(1)}, u32[]{:S(2)}, u32[]{:S(2)}) async-start(bf16[4,16,1024]{2,1,0:T(8,128)(2,1)} %bitcast.115), calls=%async_computation | async-start | bytes 262144 | tf_op jit(solution)/shard_map/while/body/eval_jaxpr/all_to_all | solution.py:99
  24.0 19.3 %all_to_all.72 = bf16[4,10,4096]{2,1,0:T(8,128)(2,1)S(1)} all-to-all(bf16[4,10,4096]{2,1,0:T(8,128)(2,1)S(1)} %reshape.338), channel_id=1, replica_groups=mesh['pipe'=2,'tensor'=4,'expert'=4] {'expert'}, dimensions={0} | all-to-all | bytes 655360 | tf_op jit(solution)/shard_map/while/body/eval_jaxpr/all_to_all | solution.py:79
  43.3 8.6 %collective-permute-done = bf16[4,10,4096]{2,1,0:T(8,128)(2,1)S(1)} collective-permute-done((bf16[4,10,4096]{2,1,0:T(8,128)(2,1)S(1)}, bf16[4,10,4096]{2,1,0:T(8,128)(2,1)S(1)}, u32[]{:S(2)}, u32[]{:S(2)}) %collective-permute-start) | collective-permute-done | bytes 327712 | tf_op jit(solution)/shard_map/while/body/eval_jaxpr/ppermute | solution.py:37
  51.9 8.6 %collective-permute-done.1 = bf16[4,10,4096]{2,1,0:T(8,128)(2,1)S(1)} collective-permute-done((bf16[4,10,4096]{2,1,0:T(8,128)(2,1)S(1)}, bf16[4,10,4096]{2,1,0:T(8,128)(2,1)S(1)}, u32[]{:S(2)}, u32[]{:S(2)}) %collective-permute-start.1) | collective-permute-done | bytes 327712 | tf_op jit(solution)/shard_map/while/body/eval_jaxpr/ppermute | solution.py:37
  60.6 8.6 %collective-permute-done.2 = bf16[4,10,4096]{2,1,0:T(8,128)(2,1)S(1)} collective-permute-done((bf16[4,10,4096]{2,1,0:T(8,128)(2,1)S(1)}, bf16[4,10,4096]{2,1,0:T(8,128)(2,1)S(1)}, u32[]{:S(2)}, u32[]{:S(2)}) %collective-permute-start.2) | collective-permute-done | bytes 327712 | tf_op jit(solution)/shard_map/while/body/eval_jaxpr/ppermute | solution.py:37
  72.9 4.5 %convolution_convert_fusion.5 = bf16[160,4096]{1,0:T(8,128)(2,1)S(1)} fusion(bf16[384,4096]{1,0:T(8,128)(2,1)} %get-tuple-element.496, bf16[160,4096]{1,0:T(8,128)(2,1)S(1)} %reshape.339, bf16[4096,384]{1,0:T(8,128)(2,1)} %get-tuple-element.495, f32[160,384]{1,0:T(8,128)S(1)} %fusion.60), kind=kOutput, calls=%fused_computation.5.clone.1 | convolution fusion | flops 1007656960 | bytes 9158656 | tf_op jit(solution)/shard_map/while/body/eval_jaxpr/dot_general | solution.py:49
  80.0 28.9 %reduce-scatter.2.cloned.1.call-done = bf16[4,10,4096]{2,1,0:T(8,128)(2,1)} async-done(((bf16[16,10,4096]{2,1,0:T(8,128)(2,1)}), bf16[4,10,4096]{2,1,0:T(8,128)(2,1)}) %reduce-scatter.2.cloned.1.call-update) | async-done | bytes 327696 | tf_op jit(solution)/shard_map/while/body/eval_jaxpr/reduce_scatter | solution.py:50
  108.8 4.6 %all-to-all-start.2 = ((bf16[4,10,4096]{2,1,0:T(8,128)(2,1)}), bf16[4,10,4096]{2,1,0:T(8,128)(2,1)S(1)}, u32[]{:S(2)}, u32[]{:S(2)}) async-start(bf16[4,10,4096]{2,1,0:T(8,128)(2,1)} %reduce-scatter.2.cloned.1.call-done), calls=%async_computation.3 | async-start | bytes 1048576 | tf_op jit(solution)/shard_map/while/body/eval_jaxpr/all_to_all | solution.py:81
  113.5 14.3 %all-to-all-done.2 = bf16[4,10,4096]{2,1,0:T(8,128)(2,1)S(1)} async-done(((bf16[4,10,4096]{2,1,0:T(8,128)(2,1)}), bf16[4,10,4096]{2,1,0:T(8,128)(2,1)S(1)}, u32[]{:S(2)}, u32[]{:S(2)}) %all-to-all-start.2) | async-done | bytes 327712 | tf_op jit(solution)/shard_map/while/body/eval_jaxpr/all_to_all | solution.py:81
  134.4 3.8 all-to-all-done.3
  139.9 3.4 collective-permute-start.3
  161.1 16.8 %all_to_all.72 = bf16[4,10,4096]{2,1,0:T(8,128)(2,1)S(1)} all-to-all(bf16[4,10,4096]{2,1,0:T(8,128)(2,1)S(1)} %reshape.338), channel_id=1, replica_groups=mesh['pipe'=2,'tensor'=4,'expert'=4] {'expert'}, dimensions={0} | all-to-all | bytes 655360 | tf_op jit(solution)/shard_map/while/body/eval_jaxpr/all_to_all | solution.py:79
  177.9 8.6 %collective-permute-done = bf16[4,10,4096]{2,1,0:T(8,128)(2,1)S(1)} collective-permute-done((bf16[4,10,4096]{2,1,0:T(8,128)(2,1)S(1)}, bf16[4,10,4096]{2,1,0:T(8,128)(2,1)S(1)}, u32[]{:S(2)}, u32[]{:S(2)}) %collective-permute-start) | collective-permute-done | bytes 327712 | tf_op jit(solution)/shard_map/while/body/eval_jaxpr/ppermute | solution.py:37
  186.5 8.6 %collective-permute-done.1 = bf16[4,10,4096]{2,1,0:T(8,128)(2,1)S(1)} collective-permute-done((bf16[4,10,4096]{2,1,0:T(8,128)(2,1)S(1)}, bf16[4,10,4096]{2,1,0:T(8,128)(2,1)S(1)}, u32[]{:S(2)}, u32[]{:S(2)}) %collective-permute-start.1) | collective-permute-done | bytes 327712 | tf_op jit(solution)/shard_map/while/body/eval_jaxpr/ppermute | solution.py:37
  195.1 8.6 %collective-permute-done.2 = bf16[4,10,4096]{2,1,0:T(8,128)(2,1)S(1)} collective-permute-done((bf16[4,10,4096]{2,1,0:T(8,128)(2,1)S(1)}, bf16[4,10,4096]{2,1,0:T(8,128)(2,1)S(1)}, u32[]{:S(2)}, u32[]{:S(2)}) %collective-permute-start.2) | collective-permute-done | bytes 327712 | tf_op jit(solution)/shard_map/while/body/eval_jaxpr/ppermute | solution.py:37
  207.4 4.5 %convolution_convert_fusion.5 = bf16[160,4096]{1,0:T(8,128)(2,1)S(1)} fusion(bf16[384,4096]{1,0:T(8,128)(2,1)} %get-tuple-element.496, bf16[160,4096]{1,0:T(8,128)(2,1)S(1)} %reshape.339, bf16[4096,384]{1,0:T(8,128)(2,1)} %get-tuple-element.495, f32[160,384]{1,0:T(8,128)S(1)} %fusion.60), kind=kOutput, calls=%fused_computation.5.clone.1 | convolution fusion | flops 1007656960 | bytes 9158656 | tf_op jit(solution)/shard_map/while/body/eval_jaxpr/dot_general | solution.py:49
  214.5 29.8 %reduce-scatter.2.cloned.1.call-done = bf16[4,10,4096]{2,1,0:T(8,128)(2,1)} async-done(((bf16[16,10,4096]{2,1,0:T(8,128)(2,1)}), bf16[4,10,4096]{2,1,0:T(8,128)(2,1)}) %reduce-scatter.2.cloned.1.call-update) | async-done | bytes 327696 | tf_op jit(solution)/shard_map/while/body/eval_jaxpr/reduce_scatter | solution.py:50
  244.3 4.6 %all-to-all-start.2 = ((bf16[4,10,4096]{2,1,0:T(8,128)(2,1)}), bf16[4,10,4096]{2,1,0:T(8,128)(2,1)S(1)}, u32[]{:S(2)}, u32[]{:S(2)}) async-start(bf16[4,10,4096]{2,1,0:T(8,128)(2,1)} %reduce-scatter.2.cloned.1.call-done), calls=%async_computation.3 | async-start | bytes 1048576 | tf_op jit(solution)/shard_map/while/body/eval_jaxpr/all_to_all | solution.py:81
  249.0 14.3 %all-to-all-done.2 = bf16[4,10,4096]{2,1,0:T(8,128)(2,1)S(1)} async-done(((bf16[4,10,4096]{2,1,0:T(8,128)(2,1)}), bf16[4,10,4096]{2,1,0:T(8,128)(2,1)S(1)}, u32[]{:S(2)}, u32[]{:S(2)}) %all-to-all-start.2) | async-done | bytes 327712 | tf_op jit(solution)/shard_map/while/body/eval_jaxpr/all_to_all | solution.py:81
  269.9 3.8 all-to-all-done.3
  275.4 3.4 collective-permute-start.3
  296.5 16.8 %all_to_all.72 = bf16[4,10,4096]{2,1,0:T(8,128)(2,1)S(1)} all-to-all(bf16[4,10,4096]{2,1,0:T(8,128)(2,1)S(1)} %reshape.338), channel_id=1, replica_groups=mesh['pipe'=2,'tensor'=4,'expert'=4] {'expert'}, dimensions={0} | all-to-all | bytes 655360 | tf_op jit(solution)/shard_map/while/body/eval_jaxpr/all_to_all | solution.py:79
  313.4 8.6 %collective-permute-done = bf16[4,10,4096]{2,1,0:T(8,128)(2,1)S(1)} collective-permute-done((bf16[4,10,4096]{2,1,0:T(8,128)(2,1)S(1)}, bf16[4,10,4096]{2,1,0:T(8,128)(2,1)S(1)}, u32[]{:S(2)}, u32[]{:S(2)}) %collective-permute-start) | collective-permute-done | bytes 327712 | tf_op jit(solution)/shard_map/while/body/eval_jaxpr/ppermute | solution.py:37
  322.0 8.6 %collective-permute-done.1 = bf16[4,10,4096]{2,1,0:T(8,128)(2,1)S(1)} collective-permute-done((bf16[4,10,4096]{2,1,0:T(8,128)(2,1)S(1)}, bf16[4,10,4096]{2,1,0:T(8,128)(2,1)S(1)}, u32[]{:S(2)}, u32[]{:S(2)}) %collective-permute-start.1) | collective-permute-done | bytes 327712 | tf_op jit(solution)/shard_map/while/body/eval_jaxpr/ppermute | solution.py:37
  330.6 8.6 %collective-permute-done.2 = bf16[4,10,4096]{2,1,0:T(8,128)(2,1)S(1)} collective-permute-done((bf16[4,10,4096]{2,1,0:T(8,128)(2,1)S(1)}, bf16[4,10,4096]{2,1,0:T(8,128)(2,1)S(1)}, u32[]{:S(2)}, u32[]{:S(2)}) %collective-permute-start.2) | collective-permute-done | bytes 327712 | tf_op jit(solution)/shard_map/while/body/eval_jaxpr/ppermute | solution.py:37
  342.9 4.5 %convolution_convert_fusion.5 = bf16[160,4096]{1,0:T(8,128)(2,1)S(1)} fusion(bf16[384,4096]{1,0:T(8,128)(2,1)} %get-tuple-element.496, bf16[160,4096]{1,0:T(8,128)(2,1)S(1)} %reshape.339, bf16[4096,384]{1,0:T(8,128)(2,1)} %get-tuple-element.495, f32[160,384]{1,0:T(8,128)S(1)} %fusion.60), kind=kOutput, calls=%fused_computation.5.clone.1 | convolution fusion | flops 1007656960 | bytes 9158656 | tf_op jit(solution)/shard_map/while/body/eval_jaxpr/dot_general | solution.py:49
  350.0 29.8 %reduce-scatter.2.cloned.1.call-done = bf16[4,10,4096]{2,1,0:T(8,128)(2,1)} async-done(((bf16[16,10,4096]{2,1,0:T(8,128)(2,1)}), bf16[4,10,4096]{2,1,0:T(8,128)(2,1)}) %reduce-scatter.2.cloned.1.call-update) | async-done | bytes 327696 | tf_op jit(solution)/shard_map/while/body/eval_jaxpr/reduce_scatter | solution.py:50
  379.8 4.6 %all-to-all-start.2 = ((bf16[4,10,4096]{2,1,0:T(8,128)(2,1)}), bf16[4,10,4096]{2,1,0:T(8,128)(2,1)S(1)}, u32[]{:S(2)}, u32[]{:S(2)}) async-start(bf16[4,10,4096]{2,1,0:T(8,128)(2,1)} %reduce-scatter.2.cloned.1.call-done), calls=%async_computation.3 | async-start | bytes 1048576 | tf_op jit(solution)/shard_map/while/body/eval_jaxpr/all_to_all | solution.py:81
  384.4 14.3 %all-to-all-done.2 = bf16[4,10,4096]{2,1,0:T(8,128)(2,1)S(1)} async-done(((bf16[4,10,4096]{2,1,0:T(8,128)(2,1)}), bf16[4,10,4096]{2,1,0:T(8,128)(2,1)S(1)}, u32[]{:S(2)}, u32[]{:S(2)}) %all-to-all-start.2) | async-done | bytes 327712 | tf_op jit(solution)/shard_map/while/body/eval_jaxpr/all_to_all | solution.py:81
  405.4 3.8 all-to-all-done.3
  410.9 3.4 collective-permute-start.3
  (239 shorter events, 92.2 us)
Async XLA Ops:
  13.4 8.9 %all-to-all-start = ((bf16[4,16,1024]{2,1,0:T(8,128)(2,1)}), bf16[4,16,1024]{2,1,0:T(8,128)(2,1)S(1)}, u32[]{:S(2)}, u32[]{:S(2)}) async-start(bf16[4,16,1024]{2,1,0:T(8,128)(2,1)} %bitcast.115), calls=%async_computation | async-start | bytes 262144 | tf_op jit(solution)/shard_map/while/body/eval_jaxpr/all_to_all | solution.py:99
  17.7 91.1 %reduce-scatter.2.cloned.1.call-start = ((), (), s32[]{:S(2)}) async-start(), calls=%async_computation.5 | async-start | bytes 2621440 | tf_op jit(solution)/shard_map/while/body/eval_jaxpr/reduce_scatter | solution.py:50
  43.3 8.6 %collective-permute-start = (bf16[4,10,4096]{2,1,0:T(8,128)(2,1)S(1)}, bf16[4,10,4096]{2,1,0:T(8,128)(2,1)S(1)}, u32[]{:S(2)}, u32[]{:S(2)}) collective-permute-start(bf16[4,10,4096]{2,1,0:T(8,128)(2,1)S(1)} %all_to_all.72), channel_id=1, source_target_pairs={{0,4},{4,8},{8,12},{12,0},{1,5},{5,9},{9,13},{13,1},{2,6},{6,10},{... | collective-permute-start | bytes 983048 | tf_op jit(solution)/shard_map/while/body/eval_jaxpr/ppermute | solution.py:37
  51.9 8.6 %collective-permute-start.1 = (bf16[4,10,4096]{2,1,0:T(8,128)(2,1)S(1)}, bf16[4,10,4096]{2,1,0:T(8,128)(2,1)S(1)}, u32[]{:S(2)}, u32[]{:S(2)}) collective-permute-start(bf16[4,10,4096]{2,1,0:T(8,128)(2,1)S(1)} %collective-permute-done), channel_id=1, source_target_pairs={{0,4},{4,8},{8,12},{12,0},{1,5},{5,9},{9,13},{13,1},{2,6},{6,10},{... | collective-permute-start | bytes 983048 | tf_op jit(solution)/shard_map/while/body/eval_jaxpr/ppermute | solution.py:37
  60.5 8.6 %collective-permute-start.2 = (bf16[4,10,4096]{2,1,0:T(8,128)(2,1)S(1)}, bf16[4,10,4096]{2,1,0:T(8,128)(2,1)S(1)}, u32[]{:S(2)}, u32[]{:S(2)}) collective-permute-start(bf16[4,10,4096]{2,1,0:T(8,128)(2,1)S(1)} %collective-permute-done.1), channel_id=1, source_target_pairs={{0,4},{4,8},{8,12},{12,0},{1,5},{5,9},{9,13},{13,1},{2,6},{6,10},{... | collective-permute-start | bytes 983048 | tf_op jit(solution)/shard_map/while/body/eval_jaxpr/ppermute | solution.py:37
  79.9 49.7 %copy-start.1 = (bf16[4,16,1024]{2,1,0:T(8,128)(2,1)S(1)}, bf16[4,16,1024]{2,1,0:T(8,128)(2,1)}, u32[]{:S(2)}) copy-start(bf16[4,16,1024]{2,1,0:T(8,128)(2,1)} %copy-done) | copy-start | bytes 393220 | tf_op jit(solution)/shard_map/while
  108.8 18.9 %all-to-all-start.2 = ((bf16[4,10,4096]{2,1,0:T(8,128)(2,1)}), bf16[4,10,4096]{2,1,0:T(8,128)(2,1)S(1)}, u32[]{:S(2)}, u32[]{:S(2)}) async-start(bf16[4,10,4096]{2,1,0:T(8,128)(2,1)} %reduce-scatter.2.cloned.1.call-done), calls=%async_computation.3 | async-start | bytes 1048576 | tf_op jit(solution)/shard_map/while/body/eval_jaxpr/all_to_all | solution.py:81
  113.4 25.7 %copy-start.2 = (bf16[2,64,1024]{2,1,0:T(8,128)(2,1)S(1)}, bf16[2,64,1024]{2,1,0:T(8,128)(2,1)}, u32[]{:S(2)}) copy-start(bf16[2,64,1024]{2,1,0:T(8,128)(2,1)} %get-tuple-element.456) | copy-start | bytes 786436 | tf_op jit(solution)/shard_map/while
  130.4 7.9 %all-to-all-start.3 = ((bf16[16,4,1024]{2,0,1:T(8,128)(2,1)}), bf16[16,4,1024]{2,0,1:T(8,128)(2,1)S(1)}, u32[]{:S(2)}, u32[]{:S(2)}) async-start(bf16[16,4,1024]{2,0,1:T(8,128)(2,1)} %fusion.63), calls=%async_computation.4 | async-start | bytes 262144 | tf_op jit(solution)/shard_map/while/body/eval_jaxpr/all_to_all | solution.py:101
  139.9 5.9 %collective-permute-start.3 = (bf16[64,1024]{1,0:T(8,128)(2,1)S(1)}, bf16[64,1024]{1,0:T(8,128)(2,1)S(1)}, u32[]{:S(2)}, u32[]{:S(2)}) collective-permute-start(bf16[64,1024]{1,0:T(8,128)(2,1)S(1)} %get-tuple-element.424), channel_id=1, source_target_pairs={{0,16},{1,17},{2,18},{3,19},{4,20},{5,21},{6,22},{7,23},{8,24},{9,... | collective-permute-start | bytes 393224 | tf_op jit(solution)/shard_map/while/body/eval_jaxpr/ppermute | solution.py:12
  151.4 7.9 %all-to-all-start = ((bf16[4,16,1024]{2,1,0:T(8,128)(2,1)}), bf16[4,16,1024]{2,1,0:T(8,128)(2,1)S(1)}, u32[]{:S(2)}, u32[]{:S(2)}) async-start(bf16[4,16,1024]{2,1,0:T(8,128)(2,1)} %bitcast.115), calls=%async_computation | async-start | bytes 262144 | tf_op jit(solution)/shard_map/while/body/eval_jaxpr/all_to_all | solution.py:99
  154.8 89.5 %reduce-scatter.2.cloned.1.call-start = ((), (), s32[]{:S(2)}) async-start(), calls=%async_computation.5 | async-start | bytes 2621440 | tf_op jit(solution)/shard_map/while/body/eval_jaxpr/reduce_scatter | solution.py:50
  177.9 8.6 %collective-permute-start = (bf16[4,10,4096]{2,1,0:T(8,128)(2,1)S(1)}, bf16[4,10,4096]{2,1,0:T(8,128)(2,1)S(1)}, u32[]{:S(2)}, u32[]{:S(2)}) collective-permute-start(bf16[4,10,4096]{2,1,0:T(8,128)(2,1)S(1)} %all_to_all.72), channel_id=1, source_target_pairs={{0,4},{4,8},{8,12},{12,0},{1,5},{5,9},{9,13},{13,1},{2,6},{6,10},{... | collective-permute-start | bytes 983048 | tf_op jit(solution)/shard_map/while/body/eval_jaxpr/ppermute | solution.py:37
  186.5 8.6 %collective-permute-start.1 = (bf16[4,10,4096]{2,1,0:T(8,128)(2,1)S(1)}, bf16[4,10,4096]{2,1,0:T(8,128)(2,1)S(1)}, u32[]{:S(2)}, u32[]{:S(2)}) collective-permute-start(bf16[4,10,4096]{2,1,0:T(8,128)(2,1)S(1)} %collective-permute-done), channel_id=1, source_target_pairs={{0,4},{4,8},{8,12},{12,0},{1,5},{5,9},{9,13},{13,1},{2,6},{6,10},{... | collective-permute-start | bytes 983048 | tf_op jit(solution)/shard_map/while/body/eval_jaxpr/ppermute | solution.py:37
  195.1 8.6 %collective-permute-start.2 = (bf16[4,10,4096]{2,1,0:T(8,128)(2,1)S(1)}, bf16[4,10,4096]{2,1,0:T(8,128)(2,1)S(1)}, u32[]{:S(2)}, u32[]{:S(2)}) collective-permute-start(bf16[4,10,4096]{2,1,0:T(8,128)(2,1)S(1)} %collective-permute-done.1), channel_id=1, source_target_pairs={{0,4},{4,8},{8,12},{12,0},{1,5},{5,9},{9,13},{13,1},{2,6},{6,10},{... | collective-permute-start | bytes 983048 | tf_op jit(solution)/shard_map/while/body/eval_jaxpr/ppermute | solution.py:37
  214.5 50.7 %copy-start.1 = (bf16[4,16,1024]{2,1,0:T(8,128)(2,1)S(1)}, bf16[4,16,1024]{2,1,0:T(8,128)(2,1)}, u32[]{:S(2)}) copy-start(bf16[4,16,1024]{2,1,0:T(8,128)(2,1)} %copy-done) | copy-start | bytes 393220 | tf_op jit(solution)/shard_map/while
  244.3 18.9 %all-to-all-start.2 = ((bf16[4,10,4096]{2,1,0:T(8,128)(2,1)}), bf16[4,10,4096]{2,1,0:T(8,128)(2,1)S(1)}, u32[]{:S(2)}, u32[]{:S(2)}) async-start(bf16[4,10,4096]{2,1,0:T(8,128)(2,1)} %reduce-scatter.2.cloned.1.call-done), calls=%async_computation.3 | async-start | bytes 1048576 | tf_op jit(solution)/shard_map/while/body/eval_jaxpr/all_to_all | solution.py:81
  248.9 20.3 %copy-start.7 = (s32[3]{0:T(128)S(1)}, s32[3]{0:T(128)}, u32[]{:S(2)}) copy-start(s32[3]{0:T(128)} %get-tuple-element.500) | copy-start | bytes 40 | tf_op jit(solution)/shard_map/while
  248.9 25.7 %copy-start.2 = (bf16[2,64,1024]{2,1,0:T(8,128)(2,1)S(1)}, bf16[2,64,1024]{2,1,0:T(8,128)(2,1)}, u32[]{:S(2)}) copy-start(bf16[2,64,1024]{2,1,0:T(8,128)(2,1)} %get-tuple-element.456) | copy-start | bytes 786436 | tf_op jit(solution)/shard_map/while
  265.9 7.9 %all-to-all-start.3 = ((bf16[16,4,1024]{2,0,1:T(8,128)(2,1)}), bf16[16,4,1024]{2,0,1:T(8,128)(2,1)S(1)}, u32[]{:S(2)}, u32[]{:S(2)}) async-start(bf16[16,4,1024]{2,0,1:T(8,128)(2,1)} %fusion.63), calls=%async_computation.4 | async-start | bytes 262144 | tf_op jit(solution)/shard_map/while/body/eval_jaxpr/all_to_all | solution.py:101
  275.4 5.9 %collective-permute-start.3 = (bf16[64,1024]{1,0:T(8,128)(2,1)S(1)}, bf16[64,1024]{1,0:T(8,128)(2,1)S(1)}, u32[]{:S(2)}, u32[]{:S(2)}) collective-permute-start(bf16[64,1024]{1,0:T(8,128)(2,1)S(1)} %get-tuple-element.424), channel_id=1, source_target_pairs={{0,16},{1,17},{2,18},{3,19},{4,20},{5,21},{6,22},{7,23},{8,24},{9,... | collective-permute-start | bytes 393224 | tf_op jit(solution)/shard_map/while/body/eval_jaxpr/ppermute | solution.py:12
  286.9 7.9 %all-to-all-start = ((bf16[4,16,1024]{2,1,0:T(8,128)(2,1)}), bf16[4,16,1024]{2,1,0:T(8,128)(2,1)S(1)}, u32[]{:S(2)}, u32[]{:S(2)}) async-start(bf16[4,16,1024]{2,1,0:T(8,128)(2,1)} %bitcast.115), calls=%async_computation | async-start | bytes 262144 | tf_op jit(solution)/shard_map/while/body/eval_jaxpr/all_to_all | solution.py:99
  290.3 89.5 %reduce-scatter.2.cloned.1.call-start = ((), (), s32[]{:S(2)}) async-start(), calls=%async_computation.5 | async-start | bytes 2621440 | tf_op jit(solution)/shard_map/while/body/eval_jaxpr/reduce_scatter | solution.py:50
  313.3 8.6 %collective-permute-start = (bf16[4,10,4096]{2,1,0:T(8,128)(2,1)S(1)}, bf16[4,10,4096]{2,1,0:T(8,128)(2,1)S(1)}, u32[]{:S(2)}, u32[]{:S(2)}) collective-permute-start(bf16[4,10,4096]{2,1,0:T(8,128)(2,1)S(1)} %all_to_all.72), channel_id=1, source_target_pairs={{0,4},{4,8},{8,12},{12,0},{1,5},{5,9},{9,13},{13,1},{2,6},{6,10},{... | collective-permute-start | bytes 983048 | tf_op jit(solution)/shard_map/while/body/eval_jaxpr/ppermute | solution.py:37
  322.0 8.6 %collective-permute-start.1 = (bf16[4,10,4096]{2,1,0:T(8,128)(2,1)S(1)}, bf16[4,10,4096]{2,1,0:T(8,128)(2,1)S(1)}, u32[]{:S(2)}, u32[]{:S(2)}) collective-permute-start(bf16[4,10,4096]{2,1,0:T(8,128)(2,1)S(1)} %collective-permute-done), channel_id=1, source_target_pairs={{0,4},{4,8},{8,12},{12,0},{1,5},{5,9},{9,13},{13,1},{2,6},{6,10},{... | collective-permute-start | bytes 983048 | tf_op jit(solution)/shard_map/while/body/eval_jaxpr/ppermute | solution.py:37
  330.6 8.6 %collective-permute-start.2 = (bf16[4,10,4096]{2,1,0:T(8,128)(2,1)S(1)}, bf16[4,10,4096]{2,1,0:T(8,128)(2,1)S(1)}, u32[]{:S(2)}, u32[]{:S(2)}) collective-permute-start(bf16[4,10,4096]{2,1,0:T(8,128)(2,1)S(1)} %collective-permute-done.1), channel_id=1, source_target_pairs={{0,4},{4,8},{8,12},{12,0},{1,5},{5,9},{9,13},{13,1},{2,6},{6,10},{... | collective-permute-start | bytes 983048 | tf_op jit(solution)/shard_map/while/body/eval_jaxpr/ppermute | solution.py:37
  350.0 50.7 %copy-start.1 = (bf16[4,16,1024]{2,1,0:T(8,128)(2,1)S(1)}, bf16[4,16,1024]{2,1,0:T(8,128)(2,1)}, u32[]{:S(2)}) copy-start(bf16[4,16,1024]{2,1,0:T(8,128)(2,1)} %copy-done) | copy-start | bytes 393220 | tf_op jit(solution)/shard_map/while
  379.8 18.9 %all-to-all-start.2 = ((bf16[4,10,4096]{2,1,0:T(8,128)(2,1)}), bf16[4,10,4096]{2,1,0:T(8,128)(2,1)S(1)}, u32[]{:S(2)}, u32[]{:S(2)}) async-start(bf16[4,10,4096]{2,1,0:T(8,128)(2,1)} %reduce-scatter.2.cloned.1.call-done), calls=%async_computation.3 | async-start | bytes 1048576 | tf_op jit(solution)/shard_map/while/body/eval_jaxpr/all_to_all | solution.py:81
  384.4 20.3 %copy-start.7 = (s32[3]{0:T(128)S(1)}, s32[3]{0:T(128)}, u32[]{:S(2)}) copy-start(s32[3]{0:T(128)} %get-tuple-element.500) | copy-start | bytes 40 | tf_op jit(solution)/shard_map/while
  384.4 25.7 %copy-start.2 = (bf16[2,64,1024]{2,1,0:T(8,128)(2,1)S(1)}, bf16[2,64,1024]{2,1,0:T(8,128)(2,1)}, u32[]{:S(2)}) copy-start(bf16[2,64,1024]{2,1,0:T(8,128)(2,1)} %get-tuple-element.456) | copy-start | bytes 786436 | tf_op jit(solution)/shard_map/while
  401.3 7.9 %all-to-all-start.3 = ((bf16[16,4,1024]{2,0,1:T(8,128)(2,1)}), bf16[16,4,1024]{2,0,1:T(8,128)(2,1)S(1)}, u32[]{:S(2)}, u32[]{:S(2)}) async-start(bf16[16,4,1024]{2,0,1:T(8,128)(2,1)} %fusion.63), calls=%async_computation.4 | async-start | bytes 262144 | tf_op jit(solution)/shard_map/while/body/eval_jaxpr/all_to_all | solution.py:101
  410.9 5.9 %collective-permute-start.3 = (bf16[64,1024]{1,0:T(8,128)(2,1)S(1)}, bf16[64,1024]{1,0:T(8,128)(2,1)S(1)}, u32[]{:S(2)}, u32[]{:S(2)}) collective-permute-start(bf16[64,1024]{1,0:T(8,128)(2,1)S(1)} %get-tuple-element.424), channel_id=1, source_target_pairs={{0,16},{1,17},{2,18},{3,19},{4,20},{5,21},{6,22},{7,23},{8,24},{9,... | collective-permute-start | bytes 393224 | tf_op jit(solution)/shard_map/while/body/eval_jaxpr/ppermute | solution.py:12
  (16 other events, 62.4 us)
Sparse Core Ops, SparseCore 0:
  79.2 29.6 reduce-scatter.1
  213.7 30.5 reduce-scatter.1
  349.2 30.5 reduce-scatter.1
